TPU v7x, 32 devices: a whole 2x2x4 slice. The times are simulated.
32 devices in a mesh: groups: 2 (over y), tm: 4 (over z), chan: 4 (over x, core).
Axes of the slice: x: 2, y: 2, z: 4, core: 2. Of those that a mesh axis runs over, the one named last changes fastest.
Arguments:
- vis: bfloat16 [8, 128, 2, 128], P(('groups', 'chan'), 'tm'), parts along dimension 0, may hold values from -6 to 6
- row_weight: bfloat16 [8, 128, 128, 128], P(('groups', 'chan'), 'tm'), parts along dimension 0, may hold values from -4 to 4
- col_weight: bfloat16 [8, 128, 128, 256], P(('groups', 'chan'), 'tm'), parts along dimension 0, may hold values from -0.5 to 0.5
- w_bin: int32 [8, 128, 1], P(('groups', 'chan'), 'tm'), parts along dimension 0, may hold values from 0 to 3; in each aligned block of 32 rows (0 to 31, 32 to 63, ..., all dimensions but the last counted through in order) at most 16 rows name the same one
- tile_col: int32 [8, 128], P(('groups', 'chan'), 'tm'), parts along dimension 0, may hold values from 0 to 15
- w_kernel: bfloat16 [8, 512, 512], P(('groups', 'tm')), parts along dimension 0, may hold values from -0.25 to 0.25
Outputs:
- grid: float32 [8, 128, 16, 512], P(('groups', 'tm'), 'chan'), parts along dimension 0
There are 2 independent parts, one for each index of `groups`. A program takes and returns all parts, laid end to end along the dimension named above; each array names one. Nothing has to cross between parts.
Inputs may be any that keep to these rules, and one draw needn't show every extreme that they name: `w_bin`: within the blocks of one device (aligned blocks of 32 along the channel-group and block dimensions taken together), no w-plane is named more than 16 times, a bound that some block reaches.
All inputs are finite; a program needn't handle non-finite values.
Results may differ from a plain program's by a relative error of at most 0.0041.
Values may be sent and summed in bfloat16 or wider, within the bound.
A program may use at most 128 MiB of HBM per device.

v0:
```python
import jax
import jax.numpy as jnp
from jax import lax
from jax.sharding import PartitionSpec as P

QW = 256
GC = 4096


def grid_group(total, weighted, columns, targets):
    patch = jnp.einsum("ghkv,gvq->gkhq", weighted, columns, preferred_element_type=jnp.float32)
    flat = patch.reshape(patch.shape[0], -1)
    return total.at[targets].add(flat, mode="drop")


def weigh_rows(rows, visibility):
    return (
        rows.astype(jnp.float32)[:, None, :, :] * visibility.astype(jnp.float32)[:, :, None, :]
    ).astype(jnp.bfloat16)


def body(vis, row_weight, col_weight, w_bin, tile_col, w_kernel):
    planes = lax.axis_size("tm")
    count = vis.shape[1]
    rows_k = row_weight.shape[2]
    width_v = vis.shape[3]
    width_q = col_weight.shape[3]
    tile_count = GC // QW
    per_plane = 2 * count // planes
    slot_total = planes * per_plane
    turns = 4
    group_len = slot_total // turns
    bins = w_bin[0, :, 0]
    tiles = tile_col[0]
    member = (bins[:, None] == jnp.arange(planes, dtype=jnp.int32)[None, :]).astype(jnp.int32)
    before = jnp.cumsum(member, axis=0) - member
    within = jnp.sum(before * member, axis=1)
    target = bins * per_plane + within
    source = (
        jnp.full((slot_total,), count, jnp.int32).at[target].set(jnp.arange(count, dtype=jnp.int32))
    )
    filled = source < count
    picked = jnp.minimum(source, count - 1)
    slot_tile = jnp.where(filled, tiles[picked], tile_count).reshape(planes, per_plane)
    columns = jnp.take(col_weight[0], picked, axis=0).reshape(planes, per_plane, width_v, width_q)
    start = jnp.zeros((tile_count, rows_k * 2 * width_q), jnp.float32)
    rows_sent = jnp.take(row_weight[0], picked, axis=0).reshape(planes, per_plane, rows_k, width_v)
    vis_sent = jnp.take(vis[0], picked, axis=0).reshape(planes, per_plane, 2, width_v)
    got_rows, got_vis, got_columns, got_tiles = (
        lax.all_to_all(rows_sent, "tm", split_axis=0, concat_axis=0, tiled=True),
        lax.all_to_all(vis_sent, "tm", split_axis=0, concat_axis=0, tiled=True),
        lax.all_to_all(columns, "tm", split_axis=0, concat_axis=0, tiled=True),
        lax.all_to_all(slot_tile, "tm", split_axis=0, concat_axis=0, tiled=True),
    )

    def step_raw(total, group):
        rows, visibility, cols, targets = group
        return (grid_group(total, weigh_rows(rows, visibility), cols, targets), None)

    groups = (
        got_rows.reshape(turns, group_len, rows_k, width_v),
        got_vis.reshape(turns, group_len, 2, width_v),
        got_columns.reshape(turns, group_len, width_v, width_q),
        got_tiles.reshape(turns, group_len),
    )
    total, _ = lax.scan(step_raw, start, groups)
    partial_value = total.reshape(tile_count, rows_k, 2 * width_q)
    share = rows_k // lax.axis_size("chan")
    summed = lax.psum(partial_value, "chan")
    mine = lax.dynamic_slice_in_dim(summed, lax.axis_index("chan") * share, share, 1)
    rounded = mine.astype(jnp.bfloat16)
    result = jnp.einsum("tkq,qr->ktr", rounded, w_kernel[0], preferred_element_type=jnp.float32)
    return result[None]


def solution(mesh):
    in_specs = (
        P(("groups", "chan"), "tm", None, None),
        P(("groups", "chan"), "tm", None, None),
        P(("groups", "chan"), "tm", None, None),
        P(("groups", "chan"), "tm", None),
        P(("groups", "chan"), "tm"),
        P(("groups", "tm"), None, None),
    )
    out_specs = P(("groups", "tm"), "chan", None, None)
    return jax.shard_map(body, mesh=mesh, in_specs=in_specs, out_specs=out_specs, check_vma=False)
```

profile of v0, /device:TPU:1, one launch (start us, length us, event | category | flops | bytes accessed | tf_op | source)
XLA Modules:
  0.0 493.3 jit_solution(4983551968529737838)
XLA Ops:
  0.0 0.0 copy-start
  0.0 0.9 fusion.8
  0.9 0.1 reduce_window_sum.11
  0.9 0.8 select_reduce_fusion
  1.8 0.7 fusion.9
  2.4 0.7 scatter_custom_fusion.1
  3.1 1.4 gather_fusion
  4.6 0.7 all_to_all.17
  5.3 5.4 %all-to-all-start = ((s32[4,1,16]{2,1,0:T(1,128)}), s32[4,1,16]{2,1,0:T(1,128)S(1)}, u32[]{:S(2)}, u32[]{:S(2)}) async-start(s32[4,1,16]{2,1,0:T(1,128)} %bitcast.13), calls=%async_computation | async-start | bytes 4096 | tf_op jit(solution)/shard_map/all_to_all | solution.py:53
  10.7 0.1 broadcast_in_dim.53
  10.8 1.4 gather_fusion.3
  12.1 0.8 broadcast_select_fusion.2
  12.9 3.4 gather_fusion.2
  16.3 0.0 all-to-all-done
  16.3 4.5 all-to-all-start.3
  20.8 3.2 broadcast_select_fusion.1
  24.1 1.3 all-to-all-done.3
  25.3 4.4 all-to-all-start.2
  29.8 0.0 copy-done
  29.8 2.8 gather_fusion.1
  32.6 6.4 %copy.14 = bf16[64,128,256]{1,2,0:T(8,128)(2,1)} copy(bf16[64,128,256]{2,1,0:T(8,128)(2,1)} %gather_fusion.1) | data formatting | bytes 8388608 | tf_op jit(solution)/shard_map/jit(_take)/gather | solution.py:45
  39.0 4.6 broadcast_select_fusion
  43.6 34.0 %all-to-all-done.2 = bf16[4,16,128,128]{3,2,1,0:T(8,128)(2,1)} async-done(((bf16[4,16,128,128]{3,2,1,0:T(8,128)(2,1)}), bf16[4,16,128,128]{3,2,1,0:T(8,128)(2,1)}, u32[]{:S(2)}, u32[]{:S(2)}) %all-to-all-start.2) | async-done | bytes 2097184 | tf_op jit(solution)/shard_map/all_to_all | solution.py:50
  77.6 5.0 %all-to-all-start.1 = ((bf16[4,16,128,256]{2,3,1,0:T(8,128)(2,1)}), bf16[4,16,128,256]{2,3,1,0:T(8,128)(2,1)}, u32[]{:S(2)}, u32[]{:S(2)}) async-start(bf16[4,16,128,256]{2,3,1,0:T(8,128)(2,1)} %broadcast_select_fusion), calls=%async_computation.1 | async-start | bytes 8388608 | tf_op jit(solution)/shard_map/all_to_all | solution.py:52
  82.6 92.6 %all-to-all-done.1 = bf16[4,16,128,256]{2,3,1,0:T(8,128)(2,1)} async-done(((bf16[4,16,128,256]{2,3,1,0:T(8,128)(2,1)}), bf16[4,16,128,256]{2,3,1,0:T(8,128)(2,1)}, u32[]{:S(2)}, u32[]{:S(2)}) %all-to-all-start.1) | async-done | bytes 4194336 | tf_op jit(solution)/shard_map/all_to_all | solution.py:52
  175.2 2.2 broadcast_in_dim.50
  177.5 227.6 %while.10 = (s32[]{:T(128)}, f32[16,65536]{1,0:T(8,128)}, s32[4,16]{1,0:T(4,128)S(1)}, bf16[4,16,128,256]{2,3,1,0:T(8,128)(2,1)}, bf16[4,16,128,128]{3,2,1,0:T(8...) while((s32[]{:T(128)}, f32[16,65536]{1,0:T(8,128)}, s32[4,16]{1,0:T(4,128)S(1)}, ...), condition=%wide.region_5.6_spmd, body=%wide.region_3.5_spmd.sunk | while | flops 270798912 | bytes 37266200 | solution.py:66
  177.5 1.1 bitcast_convert_fusion.5
  178.6 3.9 convolution_bitcast_fusion.3
  182.5 7.2 %copy.19 = f32[16,128,2,256]{3,2,1,0:T(2,128)} copy(f32[16,128,2,256]{1,3,2,0:T(8,128)} %convolution_bitcast_fusion.3) | data formatting | bytes 8388608 | tf_op jit(solution)/shard_map/while/body/eval_jaxpr/ghkv,gvq->gkhq/transpose | solution.py:11
  189.7 6.3 %reshape.160 = f32[16,65536]{1,0:T(8,128)} reshape(f32[16,128,2,256]{3,2,1,0:T(2,128)} %copy.19) | data formatting | bytes 8388608 | tf_op jit(solution)/shard_map/while/body/eval_jaxpr/reshape | solution.py:12
  196.1 38.3 %scatter_fusion = f32[16,65536]{1,0:T(8,128)} fusion(f32[16,65536]{1,0:T(8,128)} %get-tuple-element.97, s32[16]{0:T(128)S(1)} %fusion.16, f32[16,65536]{1,0:T(8,128)} %reshape.160), kind=kCustom, calls=%fused_computation.4.clone.1 | custom fusion | flops 1048576 | bytes 12582976 | tf_op jit(solution)/shard_map/while/body/eval_jaxpr/scatter-add | solution.py:13
  234.4 1.1 bitcast_convert_fusion.5
  235.6 3.9 convolution_bitcast_fusion.3
  239.5 7.2 %copy.19 = f32[16,128,2,256]{3,2,1,0:T(2,128)} copy(f32[16,128,2,256]{1,3,2,0:T(8,128)} %convolution_bitcast_fusion.3) | data formatting | bytes 8388608 | tf_op jit(solution)/shard_map/while/body/eval_jaxpr/ghkv,gvq->gkhq/transpose | solution.py:11
  246.7 6.3 %reshape.160 = f32[16,65536]{1,0:T(8,128)} reshape(f32[16,128,2,256]{3,2,1,0:T(2,128)} %copy.19) | data formatting | bytes 8388608 | tf_op jit(solution)/shard_map/while/body/eval_jaxpr/reshape | solution.py:12
  253.0 38.0 %scatter_fusion = f32[16,65536]{1,0:T(8,128)} fusion(f32[16,65536]{1,0:T(8,128)} %get-tuple-element.97, s32[16]{0:T(128)S(1)} %fusion.16, f32[16,65536]{1,0:T(8,128)} %reshape.160), kind=kCustom, calls=%fused_computation.4.clone.1 | custom fusion | flops 1048576 | bytes 12582976 | tf_op jit(solution)/shard_map/while/body/eval_jaxpr/scatter-add | solution.py:13
  291.0 1.1 bitcast_convert_fusion.5
  292.1 3.9 convolution_bitcast_fusion.3
  296.0 7.2 %copy.19 = f32[16,128,2,256]{3,2,1,0:T(2,128)} copy(f32[16,128,2,256]{1,3,2,0:T(8,128)} %convolution_bitcast_fusion.3) | data formatting | bytes 8388608 | tf_op jit(solution)/shard_map/while/body/eval_jaxpr/ghkv,gvq->gkhq/transpose | solution.py:11
  303.2 6.3 %reshape.160 = f32[16,65536]{1,0:T(8,128)} reshape(f32[16,128,2,256]{3,2,1,0:T(2,128)} %copy.19) | data formatting | bytes 8388608 | tf_op jit(solution)/shard_map/while/body/eval_jaxpr/reshape | solution.py:12
  309.6 38.6 %scatter_fusion = f32[16,65536]{1,0:T(8,128)} fusion(f32[16,65536]{1,0:T(8,128)} %get-tuple-element.97, s32[16]{0:T(128)S(1)} %fusion.16, f32[16,65536]{1,0:T(8,128)} %reshape.160), kind=kCustom, calls=%fused_computation.4.clone.1 | custom fusion | flops 1048576 | bytes 12582976 | tf_op jit(solution)/shard_map/while/body/eval_jaxpr/scatter-add | solution.py:13
  348.2 1.1 bitcast_convert_fusion.5
  349.3 3.9 convolution_bitcast_fusion.3
  353.2 7.2 %copy.19 = f32[16,128,2,256]{3,2,1,0:T(2,128)} copy(f32[16,128,2,256]{1,3,2,0:T(8,128)} %convolution_bitcast_fusion.3) | data formatting | bytes 8388608 | tf_op jit(solution)/shard_map/while/body/eval_jaxpr/ghkv,gvq->gkhq/transpose | solution.py:11
  360.4 6.3 %reshape.160 = f32[16,65536]{1,0:T(8,128)} reshape(f32[16,128,2,256]{3,2,1,0:T(2,128)} %copy.19) | data formatting | bytes 8388608 | tf_op jit(solution)/shard_map/while/body/eval_jaxpr/reshape | solution.py:12
  366.8 38.3 %scatter_fusion = f32[16,65536]{1,0:T(8,128)} fusion(f32[16,65536]{1,0:T(8,128)} %get-tuple-element.97, s32[16]{0:T(128)S(1)} %fusion.16, f32[16,65536]{1,0:T(8,128)} %reshape.160), kind=kCustom, calls=%fused_computation.4.clone.1 | custom fusion | flops 1048576 | bytes 12582976 | tf_op jit(solution)/shard_map/while/body/eval_jaxpr/scatter-add | solution.py:13
  405.0 6.5 %copy.17 = f32[2,8,128,512]{3,2,1,0:T(8,128)} copy(f32[2,8,128,512]{3,1,2,0:T(8,128)} %bitcast.63) | data formatting | bytes 8388608
  411.6 0.0 copy-start.1
  411.6 78.7 %all-reduce.1 = bf16[16,128,512]{2,1,0:T(8,128)(2,1)} all-reduce(f32[16,128,512]{2,1,0:T(8,128)} %bitcast.66), channel_id=1, replica_groups=mesh['groups'=2,'tm'=4,'chan'=4] {'chan'}, use_global_device_ids=true, to_apply=%region_6.7 | all-reduce | flops 1048576 | bytes 6291456 | tf_op jit(solution)/shard_map/psum | solution.py:69
  490.2 0.0 copy-done.1
  490.2 1.5 convolution_bitcast_fusion.1
  491.7 1.6 copy.15
  (12 shorter events, 0.1 us)
Async XLA Ops:
  0.0 29.8 %copy-start = (bf16[1,32,128,256]{3,2,1,0:T(8,128)(2,1)S(1)}, bf16[1,32,128,256]{3,2,1,0:T(8,128)(2,1)}, u32[]{:S(2)}) copy-start(bf16[1,32,128,256]{3,2,1,0:T(8,128)(2,1)} %param.10) | copy-start | bytes 6291460
  5.3 11.0 %all-to-all-start = ((s32[4,1,16]{2,1,0:T(1,128)}), s32[4,1,16]{2,1,0:T(1,128)S(1)}, u32[]{:S(2)}, u32[]{:S(2)}) async-start(s32[4,1,16]{2,1,0:T(1,128)} %bitcast.13), calls=%async_computation | async-start | bytes 4096 | tf_op jit(solution)/shard_map/all_to_all | solution.py:53
  16.3 9.0 %all-to-all-start.3 = ((bf16[4,16,2,128]{3,2,1,0:T(2,128)(2,1)}), bf16[4,16,2,128]{3,2,1,0:T(2,128)(2,1)S(1)}, u32[]{:S(2)}, u32[]{:S(2)}) async-start(bf16[4,16,2,128]{3,2,1,0:T(2,128)(2,1)} %broadcast_select_fusion.2), calls=%async_computation.3 | async-start | bytes 65536 | tf_op jit(solution)/shard_map/all_to_all | solution.py:51
  25.3 52.3 %all-to-all-start.2 = ((bf16[4,16,128,128]{3,2,1,0:T(8,128)(2,1)}), bf16[4,16,128,128]{3,2,1,0:T(8,128)(2,1)}, u32[]{:S(2)}, u32[]{:S(2)}) async-start(bf16[4,16,128,128]{3,2,1,0:T(8,128)(2,1)} %broadcast_select_fusion.1), calls=%async_computation.2 | async-start | bytes 4194304 | tf_op jit(solution)/shard_map/all_to_all | solution.py:50
  77.6 97.6 %all-to-all-start.1 = ((bf16[4,16,128,256]{2,3,1,0:T(8,128)(2,1)}), bf16[4,16,128,256]{2,3,1,0:T(8,128)(2,1)}, u32[]{:S(2)}, u32[]{:S(2)}) async-start(bf16[4,16,128,256]{2,3,1,0:T(8,128)(2,1)} %broadcast_select_fusion), calls=%async_computation.1 | async-start | bytes 8388608 | tf_op jit(solution)/shard_map/all_to_all | solution.py:52
  411.6 78.7 %copy-start.1 = (bf16[1,512,512]{2,1,0:T(8,128)(2,1)S(1)}, bf16[1,512,512]{2,1,0:T(8,128)(2,1)}, u32[]{:S(2)}) copy-start(bf16[1,512,512]{2,1,0:T(8,128)(2,1)} %param.13) | copy-start | bytes 1572868
where the time goes:
time: 495 us; the launch traced here: 493 us
  other arithmetic  169 us (34%)
  waiting for transfers between devices  128 us (26%)
  local copies, waits for them, and re-layouts  81.2 us (16%)
  blocking collectives  78.7 us (16%)
  starting transfers between devices  19.4 us (4%)
  matrix products  17.1 us (3%)
    scatter-add x4, other arithmetic, grid_group(): return total.at[targets].add(flat, mode='drop')  153 us
    all_to_all x1, waiting for transfers between devices, body(): lax.all_to_all(columns, 'tm', split_axis=0, concat_axis=0, tiled=True)  92.6 us
    psum x1, blocking collectives, body(): summed = lax.psum(partial_value, 'chan')  78.7 us
    all_to_all x1, waiting for transfers between devices, body(): lax.all_to_all(rows_sent, 'tm', split_axis=0, concat_axis=0, tiled=True)  34 us
    transpose x4, local copies, waits for them, and re-layouts, grid_group(): jnp.einsum('ghkv,gvq->gkhq', weighted, columns, preferred_element_type=jn...  28.8 us
    reshape x4, local copies, waits for them, and re-layouts, grid_group(): flat = patch.reshape(patch.shape[0], -1)  25.2 us
    dot_general x4, matrix products, grid_group(): jnp.einsum('ghkv,gvq->gkhq', weighted, columns, preferred_element_type=jn...  15.7 us
  transfers between devices with their start and end apart: 4, of which 3 were waited for; matrix products, arithmetic and copies ran while one was open for 5% of the time, Pallas kernels for 0%

commit v1 on v0

--- a/solution.py
+++ b/solution.py
@@ -66,7 +66,7 @@
     total, _ = lax.scan(step_raw, start, groups)
     partial_value = total.reshape(tile_count, rows_k, 2 * width_q)
     share = rows_k // lax.axis_size("chan")
-    summed = lax.psum(partial_value, "chan")
+    summed = jnp.sum(lax.all_gather(partial_value, "chan"), axis=0)
     mine = lax.dynamic_slice_in_dim(summed, lax.axis_index("chan") * share, share, 1)
     rounded = mine.astype(jnp.bfloat16)
     result = jnp.einsum("tkq,qr->ktr", rounded, w_kernel[0], preferred_element_type=jnp.float32)

time: 495 us -> 545 us (1.10)
  waiting for transfers between devices: 128 us -> 234 us
  blocking collectives: 78.7 us -> 0 us
  between operations: 0.07 us -> 13.5 us
  other arithmetic: 169 us -> 178 us
    all_gather x0 -> x1, waiting for transfers between devices: none -> 106 us  [body(): summed = jnp.sum(lax.all_gather(partial_value, 'chan'), axis=0)]
    psum x1 -> x0, blocking collectives: 78.7 us -> none  [body(): summed = lax.psum(partial_value, 'chan')]
    reduce_sum x0 -> x1, other arithmetic: none -> 10.1 us  [body(): summed = jnp.sum(lax.all_gather(partial_value, 'chan'), axis=0)]
  transfers between devices with their start and end apart: 4 -> 5, of which waited for: 3 -> 4; matrix products, arithmetic and copies ran while one was open for 5% -> 4% of each run, Pallas kernels for 0% -> 0%
where the time goes in v1:
time: 545 us; the launch traced here: 543 us
  waiting for transfers between devices  234 us (43%)
  other arithmetic  178 us (33%)
  local copies, waits for them, and re-layouts  81.2 us (15%)
  starting transfers between devices  19.4 us (4%)
  matrix products  17.2 us (3%)
  between operations  13.5 us (2%)
    scatter-add x4, other arithmetic, grid_group(): return total.at[targets].add(flat, mode='drop')  152 us
    all_gather x1, waiting for transfers between devices, body(): summed = jnp.sum(lax.all_gather(partial_value, 'chan'), axis=0)  106 us
    all_to_all x1, waiting for transfers between devices, body(): lax.all_to_all(columns, 'tm', split_axis=0, concat_axis=0, tiled=True)  92.5 us
    all_to_all x1, waiting for transfers between devices, body(): lax.all_to_all(rows_sent, 'tm', split_axis=0, concat_axis=0, tiled=True)  34 us
    transpose x4, local copies, waits for them, and re-layouts, grid_group(): jnp.einsum('ghkv,gvq->gkhq', weighted, columns, preferred_element_type=jn...  28.8 us
    reshape x4, local copies, waits for them, and re-layouts, grid_group(): flat = patch.reshape(patch.shape[0], -1)  25.2 us
    dot_general x4, matrix products, grid_group(): jnp.einsum('ghkv,gvq->gkhq', weighted, columns, preferred_element_type=jn...  15.7 us
  transfers between devices with their start and end apart: 5, of which 4 were waited for; matrix products, arithmetic and copies ran while one was open for 4% of the time, Pallas kernels for 0%

profile of v1, /device:TPU:1, one launch (start us, length us, event | category | flops | bytes accessed | tf_op | source)
XLA Modules:
  0.0 542.8 jit_solution(7895779885997238812)
XLA Ops:
  6.5 0.0 copy-start
  6.5 0.9 fusion.8
  7.4 0.1 reduce_window_sum.11
  7.5 0.8 select_reduce_fusion
  8.3 0.7 fusion.9
  9.0 0.7 scatter_custom_fusion.1
  9.7 1.4 gather_fusion
  11.1 0.7 all_to_all.17
  11.8 5.4 all-to-all-start
  17.2 0.1 broadcast_in_dim.53
  17.3 1.4 gather_fusion.3
  18.7 0.8 broadcast_select_fusion.2
  19.4 3.4 gather_fusion.2
  22.8 0.0 all-to-all-done
  22.8 4.5 all-to-all-start.3
  27.3 3.2 broadcast_select_fusion.1
  30.5 1.3 all-to-all-done.3
  31.8 4.4 all-to-all-start.2
  36.3 0.0 copy-done
  36.3 2.8 gather_fusion.1
  39.1 6.4 %copy.14 = bf16[64,128,256]{1,2,0:T(8,128)(2,1)} copy(bf16[64,128,256]{2,1,0:T(8,128)(2,1)} %gather_fusion.1) | data formatting | bytes 8388608 | tf_op jit(solution)/shard_map/jit(_take)/gather | solution.py:45
  45.5 4.6 broadcast_select_fusion
  50.1 34.0 %all-to-all-done.2 = bf16[4,16,128,128]{3,2,1,0:T(8,128)(2,1)} async-done(((bf16[4,16,128,128]{3,2,1,0:T(8,128)(2,1)}), bf16[4,16,128,128]{3,2,1,0:T(8,128)(2,1)}, u32[]{:S(2)}, u32[]{:S(2)}) %all-to-all-start.2) | async-done | bytes 2097184 | tf_op jit(solution)/shard_map/all_to_all | solution.py:50
  84.1 4.8 all-to-all-start.1
  89.0 0.2 all-gather.2.cloned.1.call-start
  89.2 92.5 %all-to-all-done.1 = bf16[4,16,128,256]{2,3,1,0:T(8,128)(2,1)} async-done(((bf16[4,16,128,256]{2,3,1,0:T(8,128)(2,1)}), bf16[4,16,128,256]{2,3,1,0:T(8,128)(2,1)}, u32[]{:S(2)}, u32[]{:S(2)}) %all-to-all-start.1) | async-done | bytes 4194336 | tf_op jit(solution)/shard_map/all_to_all | solution.py:52
  181.7 2.2 broadcast_in_dim.50
  183.9 226.5 %while.10 = (s32[]{:T(128)}, f32[16,65536]{1,0:T(8,128)}, s32[4,16]{1,0:T(4,128)S(1)}, bf16[4,16,128,256]{2,3,1,0:T(8,128)(2,1)}, bf16[4,16,128,128]{3,2,1,0:T(8...) while((s32[]{:T(128)}, f32[16,65536]{1,0:T(8,128)}, s32[4,16]{1,0:T(4,128)S(1)}, ...), condition=%wide.region_5.6_spmd, body=%wide.region_3.5_spmd.sunk | while | flops 270798912 | bytes 37266200 | solution.py:66
  183.9 1.1 bitcast_convert_fusion.5
  185.1 3.9 convolution_bitcast_fusion.3
  189.0 7.2 %copy.19 = f32[16,128,2,256]{3,2,1,0:T(2,128)} copy(f32[16,128,2,256]{1,3,2,0:T(8,128)} %convolution_bitcast_fusion.3) | data formatting | bytes 8388608 | tf_op jit(solution)/shard_map/while/body/eval_jaxpr/ghkv,gvq->gkhq/transpose | solution.py:11
  196.2 6.3 %reshape.156 = f32[16,65536]{1,0:T(8,128)} reshape(f32[16,128,2,256]{3,2,1,0:T(2,128)} %copy.19) | data formatting | bytes 8388608 | tf_op jit(solution)/shard_map/while/body/eval_jaxpr/reshape | solution.py:12
  202.5 38.0 %scatter_fusion = f32[16,65536]{1,0:T(8,128)} fusion(f32[16,65536]{1,0:T(8,128)} %get-tuple-element.97, s32[16]{0:T(128)S(1)} %fusion.16, f32[16,65536]{1,0:T(8,128)} %reshape.156), kind=kCustom, calls=%fused_computation.4.clone.1 | custom fusion | flops 1048576 | bytes 12582976 | tf_op jit(solution)/shard_map/while/body/eval_jaxpr/scatter-add | solution.py:13
  240.6 1.1 bitcast_convert_fusion.5
  241.7 3.9 convolution_bitcast_fusion.3
  245.7 7.2 %copy.19 = f32[16,128,2,256]{3,2,1,0:T(2,128)} copy(f32[16,128,2,256]{1,3,2,0:T(8,128)} %convolution_bitcast_fusion.3) | data formatting | bytes 8388608 | tf_op jit(solution)/shard_map/while/body/eval_jaxpr/ghkv,gvq->gkhq/transpose | solution.py:11
  252.9 6.3 %reshape.156 = f32[16,65536]{1,0:T(8,128)} reshape(f32[16,128,2,256]{3,2,1,0:T(2,128)} %copy.19) | data formatting | bytes 8388608 | tf_op jit(solution)/shard_map/while/body/eval_jaxpr/reshape | solution.py:12
  259.2 37.7 %scatter_fusion = f32[16,65536]{1,0:T(8,128)} fusion(f32[16,65536]{1,0:T(8,128)} %get-tuple-element.97, s32[16]{0:T(128)S(1)} %fusion.16, f32[16,65536]{1,0:T(8,128)} %reshape.156), kind=kCustom, calls=%fused_computation.4.clone.1 | custom fusion | flops 1048576 | bytes 12582976 | tf_op jit(solution)/shard_map/while/body/eval_jaxpr/scatter-add | solution.py:13
  296.9 1.1 bitcast_convert_fusion.5
  298.1 3.9 convolution_bitcast_fusion.3
  302.0 7.2 %copy.19 = f32[16,128,2,256]{3,2,1,0:T(2,128)} copy(f32[16,128,2,256]{1,3,2,0:T(8,128)} %convolution_bitcast_fusion.3) | data formatting | bytes 8388608 | tf_op jit(solution)/shard_map/while/body/eval_jaxpr/ghkv,gvq->gkhq/transpose | solution.py:11
  309.2 6.3 %reshape.156 = f32[16,65536]{1,0:T(8,128)} reshape(f32[16,128,2,256]{3,2,1,0:T(2,128)} %copy.19) | data formatting | bytes 8388608 | tf_op jit(solution)/shard_map/while/body/eval_jaxpr/reshape | solution.py:12
  315.5 38.3 %scatter_fusion = f32[16,65536]{1,0:T(8,128)} fusion(f32[16,65536]{1,0:T(8,128)} %get-tuple-element.97, s32[16]{0:T(128)S(1)} %fusion.16, f32[16,65536]{1,0:T(8,128)} %reshape.156), kind=kCustom, calls=%fused_computation.4.clone.1 | custom fusion | flops 1048576 | bytes 12582976 | tf_op jit(solution)/shard_map/while/body/eval_jaxpr/scatter-add | solution.py:13
  353.8 1.1 bitcast_convert_fusion.5
  355.0 3.9 convolution_bitcast_fusion.3
  358.9 7.2 %copy.19 = f32[16,128,2,256]{3,2,1,0:T(2,128)} copy(f32[16,128,2,256]{1,3,2,0:T(8,128)} %convolution_bitcast_fusion.3) | data formatting | bytes 8388608 | tf_op jit(solution)/shard_map/while/body/eval_jaxpr/ghkv,gvq->gkhq/transpose | solution.py:11
  366.1 6.3 %reshape.156 = f32[16,65536]{1,0:T(8,128)} reshape(f32[16,128,2,256]{3,2,1,0:T(2,128)} %copy.19) | data formatting | bytes 8388608 | tf_op jit(solution)/shard_map/while/body/eval_jaxpr/reshape | solution.py:12
  372.4 38.0 %scatter_fusion = f32[16,65536]{1,0:T(8,128)} fusion(f32[16,65536]{1,0:T(8,128)} %get-tuple-element.97, s32[16]{0:T(128)S(1)} %fusion.16, f32[16,65536]{1,0:T(8,128)} %reshape.156), kind=kCustom, calls=%fused_computation.4.clone.1 | custom fusion | flops 1048576 | bytes 12582976 | tf_op jit(solution)/shard_map/while/body/eval_jaxpr/scatter-add | solution.py:13
  410.4 6.5 %copy.17 = f32[2,8,128,512]{3,2,1,0:T(8,128)} copy(f32[2,8,128,512]{3,1,2,0:T(8,128)} %bitcast.64) | data formatting | bytes 8388608
  417.0 0.0 all-gather.2.cloned.1.call-update
  417.0 0.0 copy-start.2
  417.0 105.8 %all-gather.2.cloned.1.call-done = f32[4,16,128,512]{3,2,1,0:T(8,128)} async-done(((f32[1,16,128,512]{3,2,1,0:T(8,128)}), f32[4,16,128,512]{3,2,1,0:T(8,128)}) %all-gather.2.cloned.1.call-update) | async-done | bytes 16777232 | tf_op jit(solution)/shard_map/all_gather | solution.py:69
  522.8 0.0 copy-start.1
  522.8 10.1 %reduce_sum.22 = bf16[16,128,512]{2,1,0:T(8,128)(2,1)} reduce(f32[4,16,128,512]{3,2,1,0:T(8,128)} %all-gather.2.cloned.1.call-done, f32[]{:T(128)} %constant.44.clone.1), dimensions={0}, to_apply=%region_6.7 | reduce | flops 3145728 | bytes 18874372 | tf_op jit(solution)/shard_map/reduce_sum | solution.py:69
  532.9 0.0 copy-done.2
  532.9 1.5 convolution_bitcast_fusion.1
  534.4 1.6 copy.15
  536.0 0.0 copy-done.1
  (12 shorter events, 0.1 us)
Async XLA Ops:
  6.5 29.8 %copy-start = (bf16[1,32,128,256]{3,2,1,0:T(8,128)(2,1)S(1)}, bf16[1,32,128,256]{3,2,1,0:T(8,128)(2,1)}, u32[]{:S(2)}) copy-start(bf16[1,32,128,256]{3,2,1,0:T(8,128)(2,1)} %param.10) | copy-start | bytes 6291460
  11.8 11.0 %all-to-all-start = ((s32[4,1,16]{2,1,0:T(1,128)}), s32[4,1,16]{2,1,0:T(1,128)S(1)}, u32[]{:S(2)}, u32[]{:S(2)}) async-start(s32[4,1,16]{2,1,0:T(1,128)} %bitcast.13), calls=%async_computation | async-start | bytes 4096 | tf_op jit(solution)/shard_map/all_to_all | solution.py:53
  22.8 9.0 %all-to-all-start.3 = ((bf16[4,16,2,128]{3,2,1,0:T(2,128)(2,1)}), bf16[4,16,2,128]{3,2,1,0:T(2,128)(2,1)S(1)}, u32[]{:S(2)}, u32[]{:S(2)}) async-start(bf16[4,16,2,128]{3,2,1,0:T(2,128)(2,1)} %broadcast_select_fusion.2), calls=%async_computation.3 | async-start | bytes 65536 | tf_op jit(solution)/shard_map/all_to_all | solution.py:51
  31.8 52.3 %all-to-all-start.2 = ((bf16[4,16,128,128]{3,2,1,0:T(8,128)(2,1)}), bf16[4,16,128,128]{3,2,1,0:T(8,128)(2,1)}, u32[]{:S(2)}, u32[]{:S(2)}) async-start(bf16[4,16,128,128]{3,2,1,0:T(8,128)(2,1)} %broadcast_select_fusion.1), calls=%async_computation.2 | async-start | bytes 4194304 | tf_op jit(solution)/shard_map/all_to_all | solution.py:50
  84.1 97.6 %all-to-all-start.1 = ((bf16[4,16,128,256]{2,3,1,0:T(8,128)(2,1)}), bf16[4,16,128,256]{2,3,1,0:T(8,128)(2,1)}, u32[]{:S(2)}, u32[]{:S(2)}) async-start(bf16[4,16,128,256]{2,3,1,0:T(8,128)(2,1)} %broadcast_select_fusion), calls=%async_computation.1 | async-start | bytes 8388608 | tf_op jit(solution)/shard_map/all_to_all | solution.py:52
  89.0 433.9 %all-gather.2.cloned.1.call-start = ((), (), s32[]{:S(2)}) async-start(), calls=%async_computation.4 | async-start | bytes 20971520 | tf_op jit(solution)/shard_map/all_gather | solution.py:69
  417.0 115.9 %copy-start.2 = (bf16[1,512,512]{2,1,0:T(8,128)(2,1)S(1)}, bf16[1,512,512]{2,1,0:T(8,128)(2,1)}, u32[]{:S(2)}) copy-start(bf16[1,512,512]{2,1,0:T(8,128)(2,1)} %param.13) | copy-start | bytes 1572868
  522.8 13.1 %copy-start.1 = (bf16[1,32,128,256]{3,2,1,0:T(8,128)(2,1)S(1)}, bf16[1,32,128,256]{3,2,1,0:T(8,128)(2,1)}, u32[]{:S(2)}) copy-start(bf16[1,32,128,256]{3,2,1,0:T(8,128)(2,1)} %param.10) | copy-start | bytes 6291460
Sparse Core Ops, SparseCore 0:
  417.1 105.6 all-gather.1
